TPU v7x, 256 devices: a whole 4x4x8 slice. The times are simulated.
256 devices in a mesh: rep: 32 (over x, z_lo, y), shard: 8 (over z_hi, core).
Axes of the slice: x: 4, y: 4, z: 8 (z_hi: 4, z_lo: 2; z = z_hi * 2 + z_lo), core: 2. Of those that a mesh axis runs over, the one named last changes fastest.
Arguments:
- params: float32 [32, 1600, 3200], P('rep', None, 'shard'), may hold values from -6 to 6
- momentum: float32 [32, 1600, 3200], P('rep', None, 'shard'), may hold values from -6 to 6
- tokens: bfloat16 [32, 2, 1024, 1600], P('rep', None, 'shard'), may hold values from -6 to 6
- targets: bfloat16 [32, 2, 1024, 3200], P('rep', None, None, 'shard'), may hold values from -6 to 6
- blend_weight: float32 [3200], P('shard'), may hold values from 0.2 to 0.9
Outputs:
- averaged: float32 [1600, 3200], P(None, 'shard')
- blended: float32 [32, 1600, 3200], P('rep', None, 'shard')
All inputs are finite; a program needn't handle non-finite values.
Results may differ from a plain program's by a relative error of at most 0.0045.
Values may be sent and summed in bfloat16 or wider, within the bound.
A program may use at most 128 MiB of HBM per device.

v0:
```python
import jax
import jax.numpy as jnp
from jax import lax
from jax.sharding import PartitionSpec as P

D = 1600


learn_rate = 0.05
momentum_decay = 0.9


def in_blocks(shard, dim, count):
    before, after = (shard.shape[:dim], shard.shape[dim + 1 :])
    return jnp.moveaxis(shard.reshape(*before, count, -1, *after), dim, 0)


def sum_together(arrays, axis, dims):
    count = lax.axis_size(axis)
    parts = [in_blocks(a, dim, count) for a, dim in zip(arrays, dims)]
    lines = jnp.concatenate([b.reshape(count, -1) for b in parts], axis=1)
    rows = max(16, -(-lines.shape[1] // 1024) * 8)
    lines = jnp.pad(lines, ((0, 0), (0, rows * 128 - lines.shape[1]))).reshape(-1, 128)
    flat, at, gathered = (lax.psum_scatter(lines, axis, tiled=True).reshape(-1), 0, [])
    for b in parts:
        part = b[0]
        gathered.append(flat[at : at + part.size].reshape(part.shape))
        at += part.size
    return tuple(gathered)


def in_one_piece(arrays, axis, dim, along):
    ends, at = ([], 0)
    for a in arrays[:-1]:
        at += a.shape[along]
        ends.append(at)
    both = jnp.concatenate(arrays, axis=along)
    return tuple(jnp.split(lax.all_gather(both, axis, axis=dim, tiled=True), ends, axis=along))


def gelu_tanh(value):
    return jax.nn.gelu(value, approximate=True)


def local(params, momentum, tokens, targets, blend_weight):
    inputs = lax.all_gather(tokens[0], "shard", axis=1, tiled=True)
    wanted = targets[0]
    weight = params[0]
    moment = momentum[0]
    scaling = 1.0 / jnp.sqrt(jnp.float32(D))
    for local_step in range(inputs.shape[0]):
        weight_half = weight.astype(jnp.bfloat16)
        pre = jnp.dot(inputs[local_step], weight_half, preferred_element_type=jnp.float32) * scaling
        activation, pullback = jax.vjp(gelu_tanh, pre)
        (slope,) = pullback(activation - wanted[local_step].astype(jnp.float32))
        hidden_grad = (slope * scaling).astype(jnp.bfloat16)
        gradient = lax.dot_general(
            inputs[local_step],
            hidden_grad,
            (((0,), (0,)), ((), ())),
            preferred_element_type=jnp.float32,
        )
        moment = momentum_decay * moment + gradient
        weight = weight - learn_rate * moment
    replicas = lax.axis_size("rep")
    sum_weight, sum_moment = sum_together((weight, moment), "rep", (0, 0))
    averaged, mean_moment = in_one_piece(
        (sum_weight / jnp.float32(replicas), sum_moment / jnp.float32(replicas)), "rep", 0, 1
    )
    blended = blend_weight * mean_moment + (1.0 - blend_weight) * moment
    return (averaged, blended[None])


def solution(mesh):
    return jax.shard_map(
        local,
        mesh=mesh,
        in_specs=(
            P("rep", None, "shard"),
            P("rep", None, "shard"),
            P("rep", None, "shard", None),
            P("rep", None, None, "shard"),
            P("shard"),
        ),
        out_specs=(P(None, "shard"), P("rep", None, "shard")),
        check_vma=False,
    )
```

profile of v0, /device:TPU:8, one launch (start us, length us, event | category | flops | bytes accessed | tf_op | source)
XLA Modules:
  0.0 498.4 jit_solution(11711380897204350947)
XLA Ops:
  7.2 0.0 all-gather.5.cloned.1.call-start
  7.2 0.7 all-gather.5.cloned.1.call-update
  7.9 0.0 reduce-scatter.2.cloned.1.call-start
  8.0 81.2 %all-gather.5.cloned.1.call-done = bf16[1,2,1024,1600]{2,3,1,0:T(8,128)(2,1)} async-done(((bf16[1,2,128,1600]{2,3,1,0:T(8,128)(2,1)}), bf16[1,2,1024,1600]{2,3,1,0:T(8,128)(2,1)}) %all-gather.5.cloned.1.call-update) | async-done | bytes 6553616 | tf_op jit(solution)/shard_map/all_gather | solution.py:46
  89.2 10.5 %fusion = f32[1600,400]{0,1:T(8,128)} fusion(bf16[1,2,1024,1600]{2,3,1,0:T(8,128)(2,1)} %all-gather.5.cloned.1.call-done, f32[1,1600,400]{1,2,0:T(8,128)} %param.6, f32[1,1600,400]{1,2,0:T(8,128)} %param.5, bf16[1,2,1024,400]{2,3,1,0:T(8,128)(2,1)} %param.8), kind=kOutput, calls=%fused_computation.6 | convolution fusion | flops 2633600000 | bytes 15257600 | tf_op jit(solution)/shard_map/dot_general | solution.py:57
  99.6 11.8 %multiply_subtract_fusion = (f32[1600,400]{0,1:T(8,128)}, f32[1600,400]{0,1:T(8,128)}) fusion(f32[1600,400]{0,1:T(8,128)} %fusion, f32[1,1600,400]{1,2,0:T(8,128)S(1)} %copy-done.1, bf16[1,2,1024,1600]{2,3,1,0:T(8,128)(2,1)} %all-gather.5.cloned.1.call-done, bf16[1,2,1024,400]{2,3,1,0:T(8,128)(2,1)} %param.8), kind=kOutput, calls=%fused_computation.12 | convolution fusion | flops 2637440000 | bytes 23142400 | tf_op jit(solution)/shard_map/dot_general | solution.py:57
  111.4 3.3 copy.12
  114.7 2.0 reshape_reshape.7
  116.7 3.3 copy.11
  120.0 2.0 reshape_reshape.6
  122.1 5.7 %select_maximum_fusion = f32[32,40960]{1,0:T(8,128)} fusion(f32[32,20000]{1,0:T(8,128)} %reshape_reshape.7, f32[32,20000]{1,0:T(8,128)} %reshape_reshape.6), kind=kLoop, calls=%fused_computation | loop fusion | flops 5242880 | bytes 10362880 | tf_op jit(solution)/shard_map/concatenate | solution.py:21
  127.7 5.5 %reshape.29 = f32[10240,128]{1,0:T(8,128)} reshape(f32[32,40960]{1,0:T(8,128)} %select_maximum_fusion) | data formatting | bytes 10485760 | tf_op jit(solution)/shard_map/reshape | solution.py:23
  133.3 0.2 all-gather.7.cloned.1.call-start
  133.5 168.5 %reduce-scatter.2.cloned.1.call-done = f32[320,128]{1,0:T(8,128)} async-done(((f32[10240,128]{1,0:T(8,128)}), f32[320,128]{1,0:T(8,128)}) %reduce-scatter.2.cloned.1.call-update) | async-done | bytes 163856 | tf_op jit(solution)/shard_map/reduce_scatter | solution.py:24
  302.1 1.1 slice_multiply_fusion.1
  303.1 0.1 div.11
  303.3 0.1 div.13
  303.4 0.8 maximum_bitcast_fusion
  304.2 164.6 %all-gather.7.cloned.1.call-done = f32[32,50,800]{2,1,0:T(8,128)} async-done(((f32[1,50,800]{2,1,0:T(8,128)}), f32[32,50,800]{2,1,0:T(8,128)}) %all-gather.7.cloned.1.call-update) | async-done | bytes 5120016 | tf_op jit(solution)/shard_map/all_gather | solution.py:38
  468.8 5.8 %reshape.39 = f32[1600,800]{1,0:T(8,128)} reshape(f32[32,50,800]{2,1,0:T(8,128)} %all-gather.7.cloned.1.call-done) | data formatting | bytes 10240000
  474.7 5.6 %fusion.65 = (f32[1600,400]{1,0:T(8,128)}, f32[1600,400]{1,0:T(8,128)S(1)}) fusion(f32[1600,800]{1,0:T(8,128)} %reshape.39), kind=kLoop, calls=%fused_computation.82 | loop fusion | bytes 10240000 | tf_op jit(solution)/shard_map/split | solution.py:38
  480.3 4.4 copy.15
  484.7 2.7 copy.14
  487.5 4.4 add_bitcast_fusion
  (7 shorter events, 0.0 us)
Async XLA Ops:
  7.2 82.0 %all-gather.5.cloned.1.call-start = ((), (), s32[]{:S(2)}) async-start(), calls=%async_computation.2 | async-start | bytes 7372800 | tf_op jit(solution)/shard_map/all_gather | solution.py:46
  7.9 91.7 %copy-start.1 = (f32[1,1600,400]{1,2,0:T(8,128)S(1)}, f32[1,1600,400]{1,2,0:T(8,128)}, u32[]{:S(2)}) copy-start(f32[1,1600,400]{1,2,0:T(8,128)} %param.5) | copy-start | bytes 7680004
  7.9 294.2 %reduce-scatter.2.cloned.1.call-start = ((), (), s32[]{:S(2)}) async-start(), calls=%async_computation.1 | async-start | bytes 5406720 | tf_op jit(solution)/shard_map/reduce_scatter | solution.py:24
  133.3 170.9 %copy-start = (f32[400]{0:T(512)S(1)}, f32[400]{0:T(512)}, u32[]{:S(2)}) copy-start(f32[400]{0:T(512)} %param.9) | copy-start | bytes 4804
  133.3 335.5 %all-gather.7.cloned.1.call-start = ((), (), s32[]{:S(2)}) async-start(), calls=%async_computation.3 | async-start | bytes 6623232 | tf_op jit(solution)/shard_map/all_gather | solution.py:38
Sparse Core Ops, SparseCore 0:
  9.8 79.3 all-gather.4
  133.4 168.6 reduce-scatter.1
  304.4 164.3 all-gather.6
where the time goes:
time: 499 us; the launch traced here: 498 us
  waiting for transfers between devices  415 us (83%)
  local copies, waits for them, and re-layouts  35.1 us (7%)
  matrix products  22.2 us (4%)
  between operations  13.8 us (3%)
  other arithmetic  11.9 us (2%)
    reduce_scatter x1, waiting for transfers between devices, sum_together(): lax.psum_scatter(lines, axis, tiled=True).reshape(-1)  169 us
    all_gather x1, waiting for transfers between devices, in_one_piece(): lax.all_gather(both, axis, axis=dim, tiled=True)  165 us
    all_gather x1, waiting for transfers between devices, local(): inputs = lax.all_gather(tokens[0], 'shard', axis=1, tiled=True)  81.2 us
    dot_general x2, matrix products, local(): lax.dot_general(inputs[local_step], hidden_grad, (((0,), (0,)), ((), ()))...  22.2 us
    unnamed x7, local copies, waits for them, and re-layouts  13 us
  transfers between devices with their start and end apart: 3, of which 3 were waited for; matrix products, arithmetic and copies ran while one was open for 0% of the time, Pallas kernels for 0%

commit v1 on v0

v1 whole, which is shorter than its diff:
```python
import functools
import math

import jax
import jax.numpy as jnp
from jax import lax
from jax.experimental import pallas as pl
from jax.experimental.pallas import tpu as pltpu
from jax.sharding import PartitionSpec as P

D = 1600
COLS = 400
REPS = 32
LANES = 128
UNIT = 160
GROUPS = 3
TAIL = 16
TAILROWS = 200
PIECE = 64

learn_rate = 0.05
momentum_decay = 0.9

MESH = pl.DeviceIdType.MESH
F32 = jnp.float32
BF16 = jnp.bfloat16


def rem(value, count):
    return lax.rem(value, jnp.int32(count))


class Sum:
    sizes = dict(own=32, far=8, mid=8, near=16, part=8, cross=6, pair=2, other=2, full=32)

    def __init__(self, refs, rows, place, sends):
        names = list(self.sizes)
        for name, ref in zip(names, refs[: len(names)]):
            setattr(self, name, ref)
        self.send, self.recv = refs[len(names) :]
        self.rows = rows
        self.sends = sends
        self.count = 0
        self.rings, self.pair_id = place

    @classmethod
    def scratch(cls, rows):
        return [pltpu.VMEM((n, rows, LANES), BF16) for n in cls.sizes.values()] + [
            pltpu.SemaphoreType.DMA((38,)),
            pltpu.SemaphoreType.DMA((38,)),
        ]

    def go(self, slot, src, dst, device):
        copy = pltpu.make_async_remote_copy(
            src_ref=src,
            dst_ref=dst,
            send_sem=self.send.at[slot],
            recv_sem=self.recv.at[slot],
            device_id=device,
            device_id_type=MESH,
        )
        copy.start()
        self.sends.append(copy)

    def got(self, slot, dst):
        pltpu.make_async_remote_copy(
            src_ref=dst,
            dst_ref=dst,
            send_sem=self.send.at[slot],
            recv_sem=self.recv.at[slot],
            device_id=self.pair_id,
            device_id_type=MESH,
        ).wait_recv()

    def halves(self):
        for h in range(2):
            (i1, peer1), (i2, peer2) = self.rings if h == 0 else self.rings[::-1]
            yield h, i1, peer1, i2, peer2

    def s1(self):
        for h, i1, peer1, i2, peer2 in self.halves():
            base = 16 * h + 4 * rem(i1 + 2, 4)
            self.go(2 * h, self.own.at[pl.ds(base, 2)], self.far.at[pl.ds(4 * h, 2)], peer1(1))
            self.go(2 * h + 1, self.own.at[pl.ds(base + 2, 2)], self.far.at[pl.ds(4 * h + 2, 2)], peer1(3))
        for h, i1, peer1, i2, peer2 in self.halves():
            right = 16 * h + 4 * rem(i1 + 1, 4)
            left = 16 * h + 4 * rem(i1 + 3, 4)
            self.go(4 + 2 * h, self.own.at[pl.ds(right + 2, 2)], self.near.at[pl.ds(8 * h + 2, 2)], peer1(1))
            self.go(5 + 2 * h, self.own.at[pl.ds(left, 2)], self.near.at[pl.ds(8 * h + 4, 2)], peer1(3))

    def s2(self):
        for h, i1, peer1, i2, peer2 in self.halves():
            right = 16 * h + 4 * rem(i1 + 1, 4)
            left = 16 * h + 4 * rem(i1 + 3, 4)
            for side, first, at in ((0, right, 0), (1, left + 2, 6)):
                mid = self.mid.at[pl.ds(4 * h + 2 * side, 2)]
                self.got(2 * h + side, self.far.at[pl.ds(4 * h + 2 * side, 2)])
                mid[...] = (
                    self.own[pl.ds(first, 2)].astype(F32) + self.far[pl.ds(4 * h + 2 * side, 2)].astype(F32)
                ).astype(BF16)
                self.go(8 + 2 * h + side, mid, self.near.at[pl.ds(8 * h + at, 2)], peer1(1 + 2 * side))

    def s3(self):
        for h, i1, peer1, i2, peer2 in self.halves():
            self.got(4 + 2 * h, self.near.at[pl.ds(8 * h + 2, 2)])
            self.got(5 + 2 * h, self.near.at[pl.ds(8 * h + 4, 2)])
            self.got(8 + 2 * h, self.near.at[pl.ds(8 * h, 2)])
            self.got(9 + 2 * h, self.near.at[pl.ds(8 * h + 6, 2)])
            mine = 16 * h + 4 * i1
            self.part[pl.ds(4 * h, 4)] = (
                self.own[pl.ds(mine, 4)].astype(F32)
                + self.near[pl.ds(8 * h, 4)].astype(F32)
                + self.near[pl.ds(8 * h + 4, 4)].astype(F32)
            ).astype(BF16)
            for d in range(1, 4):
                self.go(
                    12 + 3 * h + d - 1,
                    self.part.at[pl.ds(4 * h + rem(i2 + d, 4), 1)],
                    self.cross.at[pl.ds(3 * h + d - 1, 1)],
                    peer2(d),
                )

    def s4(self):
        for h, i1, peer1, i2, peer2 in self.halves():
            total = self.part[4 * h + i2].astype(F32)
            for d in range(1, 4):
                self.got(12 + 3 * h + d - 1, self.cross.at[pl.ds(3 * h + d - 1, 1)])
                total = total + self.cross[3 * h + d - 1].astype(F32)
            self.pair[h] = total.astype(BF16)
            self.go(18 + h, self.pair.at[pl.ds(h, 1)], self.other.at[pl.ds(h, 1)], self.pair_id)

    def s5(self):
        for h, i1, peer1, i2, peer2 in self.halves():
            self.got(18 + h, self.other.at[pl.ds(h, 1)])
            mine = 16 * h + 4 * i1 + i2
            self.full[mine] = (self.pair[h].astype(F32) + self.other[h].astype(F32)).astype(BF16)
            for d in range(1, 4):
                self.go(20 + 3 * h + d - 1, self.full.at[pl.ds(mine, 1)], self.full.at[pl.ds(mine, 1)], peer2(d))

    def s6(self):
        for h, i1, peer1, i2, peer2 in self.halves():
            mine = 16 * h + 4 * i1
            for d in range(1, 4):
                self.got(20 + 3 * h + d - 1, self.full.at[pl.ds(mine + rem(i2 + 4 - d, 4), 1)])
            low, high = self.full.at[pl.ds(mine, 2)], self.full.at[pl.ds(mine + 2, 2)]
            self.go(26 + 6 * h, low, low, peer1(1))
            self.go(27 + 6 * h, high, high, peer1(3))
            self.go(28 + 6 * h, high, high, peer1(1))
            self.go(29 + 6 * h, low, low, peer1(3))

    def s7(self):
        for h, i1, peer1, i2, peer2 in self.halves():
            low = self.full.at[pl.ds(16 * h + 4 * rem(i1 + 3, 4), 2)]
            high = self.full.at[pl.ds(16 * h + 4 * rem(i1 + 1, 4) + 2, 2)]
            self.got(26 + 6 * h, low)
            self.go(30 + 6 * h, low, low, peer1(1))
            self.got(27 + 6 * h, high)
            self.go(31 + 6 * h, high, high, peer1(3))

    def s8(self):
        for h, i1, peer1, i2, peer2 in self.halves():
            self.got(28 + 6 * h, self.full.at[pl.ds(16 * h + 4 * rem(i1 + 3, 4) + 2, 2)])
            self.got(29 + 6 * h, self.full.at[pl.ds(16 * h + 4 * rem(i1 + 1, 4), 2)])
        for h, i1, peer1, i2, peer2 in self.halves():
            far = 16 * h + 4 * rem(i1 + 2, 4)
            self.got(30 + 6 * h, self.full.at[pl.ds(far, 2)])
            self.got(31 + 6 * h, self.full.at[pl.ds(far + 2, 2)])


def pack(source, own, at, narrow):
    def body(i, carry):
        rows = pl.ds(pl.multiple_of(i * UNIT, UNIT), UNIT)
        for g in range(GROUPS):
            own[10 * g + i, at : at + UNIT, :] = source[rows, LANES * g : LANES * (g + 1)].astype(BF16)
        return carry

    lax.fori_loop(0, 10, body, 0)
    narrow[:, :TAIL] = source[:, LANES * GROUPS :]
    lane = lax.broadcasted_iota(jnp.int32, (TAILROWS, LANES), 1) // TAIL
    packed = jnp.zeros((TAILROWS, LANES), F32)
    for b in range(8):
        part = narrow[TAILROWS * b : TAILROWS * (b + 1), :]
        packed = jnp.where(lane == b, pltpu.roll(part, TAIL * b, 1) if b else part, packed)
    own[30, at : at + UNIT, :] = packed[:UNIT].astype(BF16)
    own[31, at : at + UNIT, :] = jnp.concatenate(
        [packed[UNIT:], jnp.zeros((2 * UNIT - TAILROWS, LANES), F32)], axis=0
    ).astype(BF16)


def kernel(
    w_hbm, m_hbm, tok_hbm, tgt_hbm, bw_ref, avg_hbm, bl_hbm,
    tok, tgt, w, m, g, half, narrow, avg, bl, hg, tsend, trecv, lsem, *sum_refs,
):
    rep, shard = lax.axis_index("rep"), lax.axis_index("shard")
    x, zl, y = rep // 8, rem(rep // 4, 2), rem(rep, 4)
    zh, core = shard // 2, rem(shard, 2)
    right = (rep, 2 * rem(zh + 1, 4) + core)
    left = (rep, 2 * rem(zh + 3, 4) + core)
    partner = (rep, 2 * zh + 1 - core)
    pair_id = (8 * x + 4 * (1 - zl) + y, shard)

    def along_x(d):
        return (8 * rem(x + d, 4) + 4 * zl + y, shard)

    def along_y(d):
        return (8 * x + 4 * zl + rem(y + d, 4), shard)

    sends = []
    place = (((x, along_x), (y, along_y)), pair_id)
    per = len(Sum.sizes) + 2
    first = Sum(sum_refs[:per], 2 * UNIT, place, sends)
    second = Sum(sum_refs[per : 2 * per], UNIT, place, sends)
    third = Sum(sum_refs[2 * per :], UNIT, place, sends)

    loads = [
        pltpu.make_async_copy(tok_hbm.at[0], tok.at[0, 0, pl.ds(2 * core, 2)], lsem.at[0]),
        pltpu.make_async_copy(w_hbm, w, lsem.at[1]),
        pltpu.make_async_copy(m_hbm, m, lsem.at[2]),
        pltpu.make_async_copy(tgt_hbm, tgt, lsem.at[3]),
        pltpu.make_async_copy(tok_hbm.at[1], tok.at[1, 0, pl.ds(2 * core, 2)], lsem.at[4]),
    ]
    for load in loads:
        load.start()
    narrow[...] = jnp.zeros_like(narrow)

    peers = [right, left, partner, pair_id] + [f(d) for f in (along_x, along_y) for d in (1, 2, 3)]
    barrier = pltpu.get_barrier_semaphore()
    for peer in peers:
        pl.semaphore_signal(barrier, inc=1, device_id=peer, device_id_type=MESH)
    pl.semaphore_wait(barrier, len(peers))

    def move(step, slot, src, dst, batch, j, device):
        copy = pltpu.make_async_remote_copy(
            src_ref=src,
            dst_ref=dst,
            send_sem=tsend.at[step, slot],
            recv_sem=trecv.at[step, batch, j],
            device_id=device,
            device_id_type=MESH,
        )
        copy.start()
        sends.append(copy)

    def came(step, batch, j, dst):
        pltpu.make_async_remote_copy(
            src_ref=dst,
            dst_ref=dst,
            send_sem=tsend.at[step, 0],
            recv_sem=trecv.at[step, batch, j],
            device_id=partner,
            device_id_type=MESH,
        ).wait_recv()

    def send_own(step):
        lower, upper = tok.at[step, 0, 2 * core], tok.at[step, 0, 2 * core + 1]
        move(step, 0, lower, tok.at[step, 1, core], 1, core, right)
        move(step, 1, upper, tok.at[step, 1, 2 + core], 1, 2 + core, left)
        move(step, 2, upper, tok.at[step, 2, core], 2, core, right)
        move(step, 3, lower, tok.at[step, 2, 2 + core], 2, 2 + core, left)
        both = tok.at[step, 0, pl.ds(2 * core, 2)]
        move(step, 4, both, both, 0, 2 * core, partner)

    def receive(step, batch):
        if batch == 0:
            came(step, 0, 2 * (1 - core), tok.at[step, 0, pl.ds(2 * (1 - core), 2)])
            return
        for side, onward in ((0, right), (1, left)):
            j = 2 * side + core
            here = tok.at[step, batch, j]
            came(step, batch, j, here)
            if batch == 1:
                move(step, 5 + side, here, tok.at[step, 3, j], 3, j, onward)
            move(step, 5 + 2 * batch + side, here, here, batch, j, partner)

    def receive_partner(step, batch):
        if batch:
            for side in range(2):
                j = 2 * side + 1 - core
                came(step, batch, j, tok.at[step, batch, j])

    scaling = 1.0 / math.sqrt(D)
    root = math.sqrt(2.0 / math.pi)

    def compute(step, batch):
        block = tok[step, batch].reshape(4 * PIECE, D)
        pre = jnp.dot(block, half[...], preferred_element_type=F32) * scaling
        if batch == 0:
            starts = [zh * 256 + 64 * j for j in range(4)]
        else:
            near = {1: (3, 1), 2: (3, 1), 3: (2, 2)}[batch]
            add = {1: (0, 64), 2: (64, 0), 3: (0, 64)}[batch]
            starts = [
                rem(zh + near[side], 4) * 256 + 128 * c + add[side] for side in range(2) for c in range(2)
            ]
        for j, start in enumerate(starts):
            value = pre[PIECE * j : PIECE * (j + 1)]
            wanted = tgt[step, pl.ds(pl.multiple_of(start, PIECE), PIECE), :].astype(F32)
            square = value * value
            curve = jnp.tanh(root * value * (1.0 + 0.044715 * square))
            gate = 0.5 * (1.0 + curve)
            slope = gate + 0.5 * value * (1.0 - curve * curve) * (root * (1.0 + 3 * 0.044715 * square))
            hg[PIECE * j : PIECE * (j + 1), :] = ((value * gate - wanted) * slope * scaling).astype(BF16)
        part = lax.dot_general(block, hg[...], (((0,), (0,)), ((), ())), preferred_element_type=F32)
        if batch == 0:
            g[...] = part
        else:
            g[...] += part

    loads[0].wait()
    send_own(0)
    loads[1].wait()
    half[...] = w[...].astype(BF16)
    pack(w, first.own, 0, narrow)
    loads[2].wait()
    pack(m, first.own, UNIT, narrow)
    first.s1()
    loads[3].wait()
    loads[4].wait()

    receive(0, 0)
    compute(0, 0)
    first.s2()

    receive(0, 1)
    send_own(1)
    receive_partner(0, 1)
    compute(0, 1)
    first.s3()
    first.s4()

    receive(0, 2)
    receive_partner(0, 2)
    compute(0, 2)
    first.s5()
    first.s6()

    receive(0, 3)
    receive_partner(0, 3)
    compute(0, 3)
    m[...] = momentum_decay * m[...] + g[...]
    half[...] = (w[...] - learn_rate * m[...]).astype(BF16)
    pack(g, second.own, 0, narrow)
    second.s1()

    receive(1, 0)
    compute(1, 0)
    first.s7()
    second.s2()

    receive(1, 1)
    receive_partner(1, 1)
    compute(1, 1)
    first.s8()
    second.s3()
    second.s4()

    receive(1, 2)
    receive_partner(1, 2)
    compute(1, 2)
    second.s5()
    second.s6()

    receive(1, 3)
    receive_partner(1, 3)
    compute(1, 3)
    pack(g, third.own, 0, narrow)
    third.s1()

    second.s7()
    m[...] = momentum_decay * m[...] + g[...]
    share = 1.0 / REPS
    second.s8()
    third.s2()

    def sums(unit, rows):
        w0 = first.full[unit, :UNIT][rows].astype(F32)
        m0 = first.full[unit, UNIT:][rows].astype(F32)
        g1 = second.full[unit][rows].astype(F32)
        d = momentum_decay
        average = w0 - learn_rate * ((d + d * d) * m0 + (1.0 + d) * g1)
        return average * share, (d * d * m0 + d * g1) * share

    every = slice(None)

    def base(i, carry):
        rows = pl.ds(pl.multiple_of(i * UNIT, UNIT), UNIT)
        for k in range(GROUPS):
            columns = slice(LANES * k, LANES * (k + 1))
            average, mean = sums(10 * k + i, every)
            part = bw_ref[:, columns]
            avg[rows, columns] = average
            bl[rows, columns] = part * mean + (1.0 - part) * m[rows, columns]
        return carry

    lax.fori_loop(0, 10, base, 0)
    last = slice(LANES * GROUPS, COLS)
    ends = [sums(30, every), sums(31, slice(0, TAILROWS - UNIT))]
    average, mean = (jnp.concatenate([a, b], axis=0) for a, b in zip(*ends))
    part = bw_ref[:, last]
    for b in range(8):
        rows = slice(TAILROWS * b, TAILROWS * (b + 1))
        shift = LANES - TAIL * b
        avg[rows, last] = (pltpu.roll(average, shift, 1) if b else average)[:, :TAIL]
        bl[rows, last] = part * (pltpu.roll(mean, shift, 1) if b else mean)[:, :TAIL] + (1.0 - part) * m[rows, last]

    third.s3()
    third.s4()
    third.s5()
    third.s6()
    third.s7()
    third.s8()

    def finish(i, carry):
        rows = pl.ds(pl.multiple_of(i * UNIT, UNIT), UNIT)
        for k in range(GROUPS):
            columns = slice(LANES * k, LANES * (k + 1))
            total = third.full[10 * k + i].astype(F32) * share
            avg[rows, columns] = avg[rows, columns] - learn_rate * total
            bl[rows, columns] = bl[rows, columns] + bw_ref[:, columns] * total
        return carry

    lax.fori_loop(0, 10, finish, 0)
    total = jnp.concatenate(
        [third.full[30].astype(F32), third.full[31, : TAILROWS - UNIT].astype(F32)], axis=0
    ) * share
    for b in range(8):
        rows = slice(TAILROWS * b, TAILROWS * (b + 1))
        piece = (pltpu.roll(total, LANES - TAIL * b, 1) if b else total)[:, :TAIL]
        avg[rows, last] = avg[rows, last] - learn_rate * piece
        bl[rows, last] = bl[rows, last] + part * piece
    outs = [
        pltpu.make_async_copy(avg, avg_hbm, lsem.at[0]),
        pltpu.make_async_copy(bl, bl_hbm, lsem.at[1]),
    ]
    for out in outs:
        out.start()
    for copy in sends:
        copy.wait_send()
    for out in outs:
        out.wait()


def local(params, momentum, tokens, targets, blend_weight):
    anywhere = pl.BlockSpec(memory_space=pl.ANY)
    averaged, blended = pl.pallas_call(
        kernel,
        out_shape=[jax.ShapeDtypeStruct((D, COLS), F32)] * 2,
        in_specs=[anywhere] * 4 + [pl.BlockSpec(memory_space=pltpu.VMEM)],
        out_specs=[anywhere] * 2,
        scratch_shapes=[
            pltpu.VMEM((2, 4, 4, PIECE, D), BF16),
            pltpu.VMEM((2, 1024, COLS), BF16),
            pltpu.VMEM((D, COLS), F32),
            pltpu.VMEM((D, COLS), F32),
            pltpu.VMEM((D, COLS), F32),
            pltpu.VMEM((D, COLS), BF16),
            pltpu.VMEM((D, LANES), F32),
            pltpu.VMEM((D, COLS), F32),
            pltpu.VMEM((D, COLS), F32),
            pltpu.VMEM((4 * PIECE, COLS), BF16),
            pltpu.SemaphoreType.DMA((2, 13)),
            pltpu.SemaphoreType.DMA((2, 4, 4)),
            pltpu.SemaphoreType.DMA((5,)),
            *Sum.scratch(2 * UNIT),
            *Sum.scratch(UNIT),
            *Sum.scratch(UNIT),
        ],
        compiler_params=pltpu.CompilerParams(
            collective_id=0, has_side_effects=True, vmem_limit_bytes=67043328
        ),
        name="window",
    )(
        params[0],
        momentum[0],
        tokens.reshape(2, 2, PIECE, D),
        targets[0],
        blend_weight.reshape(1, COLS),
    )
    return averaged, blended[None]


def solution(mesh):
    return jax.shard_map(
        local,
        mesh=mesh,
        in_specs=(
            P("rep", None, "shard"),
            P("rep", None, "shard"),
            P("rep", None, "shard", None),
            P("rep", None, None, "shard"),
            P("shard"),
        ),
        out_specs=(P(None, "shard"), P("rep", None, "shard")),
        check_vma=False,
    )
```

time: 499 us -> 158 us (0.32)
  waiting for transfers between devices: 415 us -> 0 us
  Pallas kernels: 0 us -> 136 us
  matrix products: 22.2 us -> 0 us
  local copies, waits for them, and re-layouts: 35.1 us -> 20.8 us
  between operations: 13.8 us -> 0.66 us
  other arithmetic: 11.9 us -> 0 us
    all_gather x2 -> x0, waiting for transfers between devices: 246 us -> none  [the longest x1 165 us: in_one_piece(): lax.all_gather(both, axis, axis=dim, tiled=True)]
    reduce_scatter x1 -> x0, waiting for transfers between devices: 169 us -> none  [sum_together(): lax.psum_scatter(lines, axis, tiled=True).reshape(-1)]
    pallas_call x0 -> x1, Pallas kernels: none -> 136 us  [local(): pl.pallas_call(kernel, out_shape=[jax.ShapeDtypeStruct((D, COLS), F32)] *...]
    dot_general x2 -> x0, matrix products: 22.2 us -> none  [local(): lax.dot_general(inputs[local_step], hidden_grad, (((0,), (0,)), ((), ()))...]
    unnamed x7 -> x10, local copies, waits for them, and re-layouts: 13 us -> 20.8 us
    concatenate x1 -> x0, other arithmetic: 5.67 us -> none  [sum_together(): lines = jnp.concatenate([b.reshape(count, -1) for b in parts], axis=1)]
    split x1 -> x0, local copies, waits for them, and re-layouts: 5.62 us -> none  [in_one_piece(): jnp.split(lax.all_gather(both, axis, axis=dim, tiled=True), ends, axis=al...]
    reshape x1 -> x0, local copies, waits for them, and re-layouts: 5.53 us -> none  [sum_together(): jnp.pad(lines, ((0, 0), (0, rows * 128 - lines.shape[1]))).reshape(-1, 128)]
  transfers between devices with their start and end apart: 3 -> 0, of which waited for: 3 -> 0; matrix products, arithmetic and copies ran while one was open for 0% -> 0% of each run, Pallas kernels for 0% -> 0%
where the time goes in v1:
time: 158 us
  Pallas kernels  136 us (86%)
  local copies, waits for them, and re-layouts  20.8 us (13%)
    pallas_call x1, Pallas kernels, local(): pl.pallas_call(kernel, out_shape=[jax.ShapeDtypeStruct((D, COLS), F32)] *...  136 us
    unnamed x10, local copies, waits for them, and re-layouts  20.8 us

profile of v1, /device:TPU:8, one launch (start us, length us, event | category | flops | bytes accessed | tf_op | source)
XLA Modules:
  0.0 157.5 jit_solution(4696212025089608379)
XLA Ops:
  0.6 0.0 copy-start.1
  0.6 2.3 %copy.9 = bf16[1,2,128,1600]{3,2,1,0:T(8,128)(2,1)} copy(bf16[1,2,128,1600]{2,3,1,0:T(8,128)(2,1)} %param.7) | data formatting | bytes 1638400 | tf_op args[2]
  3.0 3.8 %copy.10 = bf16[1,2,1024,400]{3,2,1,0:T(8,128)(2,1)} copy(bf16[1,2,1024,400]{2,3,1,0:T(8,128)(2,1)} %param.8) | data formatting | bytes 3276800 | tf_op args[3]
  6.7 0.0 copy-done.1
  6.7 2.9 %copy.7 = f32[1,1600,400]{2,1,0:T(8,128)} copy(f32[1,1600,400]{1,2,0:T(8,128)S(1)} %copy-done.1) | data formatting | bytes 5120000 | tf_op args[0]
  9.7 4.4 %copy.8 = f32[1,1600,400]{2,1,0:T(8,128)} copy(f32[1,1600,400]{1,2,0:T(8,128)} %param.6) | data formatting | bytes 5120000 | tf_op args[1]
  14.1 136.1 %window.1 = (f32[1600,400]{1,0:T(8,128)}, f32[1600,400]{1,0:T(8,128)}) custom-call(f32[1600,400]{1,0:T(8,128)} %bitcast.6, f32[1600,400]{1,0:T(8,128)} %bitcast.7, bf16[2,2,64,1600]{3,2,1,0:T(8,128)(2,1)} %bitcast.9, bf16[2,1024,400]{2,1,0:T(8,128)(2,1)} %bitcast.8, f32[1,400]{1,0:T(1,128)} %bitcast.11), custom_call_target="tpu_custom_call" | custom-call | tf_op jit(solution)/shard_map/window/pallas_call | solution.py:445
  150.2 0.0 copy-start
  150.2 4.6 %copy.11 = f32[1600,400]{0,1:T(8,128)} copy(f32[1600,400]{1,0:T(8,128)} %get-tuple-element.6) | data formatting | bytes 5120000
  154.8 0.0 copy-done
  154.8 2.7 %copy.12 = f32[1,1600,400]{1,2,0:T(8,128)} copy(f32[1,1600,400]{2,1,0:T(8,128)S(1)} %bitcast.10) | data formatting | bytes 5120000
Async XLA Ops:
  0.6 6.1 %copy-start.1 = (f32[1,1600,400]{1,2,0:T(8,128)S(1)}, f32[1,1600,400]{1,2,0:T(8,128)}, u32[]{:S(2)}) copy-start(f32[1,1600,400]{1,2,0:T(8,128)} %param.5) | copy-start | bytes 7680004
  150.2 4.6 %copy-start = (f32[1600,400]{1,0:T(8,128)S(1)}, f32[1600,400]{1,0:T(8,128)}, u32[]{:S(2)}) copy-start(f32[1600,400]{1,0:T(8,128)} %get-tuple-element.5) | copy-start | bytes 7680004

commit v2 on v0

v2 whole, which is shorter than its diff:
```python
import functools
import math

import jax
import jax.numpy as jnp
from jax import lax
from jax.experimental import pallas as pl
from jax.experimental.pallas import tpu as pltpu
from jax.sharding import PartitionSpec as P

D = 1600
COLS = 400
REPS = 32
LANES = 128
SUB = 80
GROUPS = 12
TAIL = 64
TAILROWS = 200
TOKS = 128

learn_rate = 0.05
momentum_decay = 0.9

MESH = pl.DeviceIdType.MESH
F32 = jnp.float32
BF16 = jnp.bfloat16
LAST = slice(GROUPS * LANES, D)


def rem(value, count):
    return lax.rem(value, jnp.int32(count))


class Sum:
    sizes = dict(own=32, far=8, mid=8, near=16, part=8, cross=6, pair=2, other=2, full=32)

    def __init__(self, refs, place, per, wide):
        self.flight = []
        self.per = per
        names = list(self.sizes)
        for name, ref in zip(names, refs[: len(names)]):
            setattr(self, name, ref)
        self.send, self.recv = refs[len(names) :]
        self.wide = wide
        self.rings, self.pair_id = place

    @classmethod
    def scratch(cls, per, wide):
        inner = ("part", "cross")
        return [
            pltpu.VMEM((per * n, SUB, LANES), wide if name in inner else BF16) for name, n in cls.sizes.items()
        ] + [pltpu.SemaphoreType.DMA((9,)), pltpu.SemaphoreType.DMA((7,))]

    def units(self, first, count):
        return pl.ds(self.per * first, self.per * count)

    def copy(self, stage, kind, src, dst, device):
        return pltpu.make_async_remote_copy(
            src_ref=src,
            dst_ref=dst,
            send_sem=self.send.at[stage],
            recv_sem=self.recv.at[kind],
            device_id=device,
            device_id_type=MESH,
        )

    def go(self, stage, kind, src, dst, device):
        self.copy(stage, kind, src, dst, device).start()
        if stage not in self.flight:
            self.flight.append(stage)

    def flush(self):
        for stage in self.flight:
            source, count = ((self.own, 8), (self.own, 8), (self.mid, 8), (self.part, 6), (self.pair, 2), (self.full, 6), (self.full, 8), (self.full, 8), (self.full, 8))[stage]
            all_sent = source.at[self.units(0, count)]
            self.copy(stage, 0, all_sent, all_sent, self.pair_id).wait_send()
        self.flight = []

    def got(self, kind, ref, count):
        everything = ref.at[self.units(0, count)]
        self.copy(0, kind, everything, everything, self.pair_id).wait_recv()

    def halves(self):
        for h in range(2):
            (i1, peer1), (i2, peer2) = self.rings if h == 0 else self.rings[::-1]
            yield h, i1, peer1, i2, peer2

    def s1(self):
        u = self.units
        for h, i1, peer1, i2, peer2 in self.halves():
            base = 16 * h + 4 * rem(i1 + 2, 4)
            self.go(0, 0, self.own.at[u(base, 2)], self.far.at[u(4 * h, 2)], peer1(1))
            self.go(0, 0, self.own.at[u(base + 2, 2)], self.far.at[u(4 * h + 2, 2)], peer1(3))

    def s1b(self):
        u = self.units
        for h, i1, peer1, i2, peer2 in self.halves():
            right = 16 * h + 4 * rem(i1 + 1, 4)
            left = 16 * h + 4 * rem(i1 + 3, 4)
            self.go(1, 1, self.own.at[u(right + 2, 2)], self.near.at[u(8 * h + 2, 2)], peer1(1))
            self.go(1, 1, self.own.at[u(left, 2)], self.near.at[u(8 * h + 4, 2)], peer1(3))

    def s2(self):
        u = self.units
        self.got(0, self.far, 8)
        for h, i1, peer1, i2, peer2 in self.halves():
            right = 16 * h + 4 * rem(i1 + 1, 4)
            left = 16 * h + 4 * rem(i1 + 3, 4)
            for side, first, at in ((0, right, 0), (1, left + 2, 6)):
                here = u(4 * h + 2 * side, 2)
                self.mid[here] = (self.own[u(first, 2)].astype(F32) + self.far[here].astype(F32)).astype(BF16)
                self.go(2, 1, self.mid.at[here], self.near.at[u(8 * h + at, 2)], peer1(1 + 2 * side))

    def s3(self):
        u = self.units
        self.got(1, self.near, 16)
        for h, i1, peer1, i2, peer2 in self.halves():
            mine = 16 * h + 4 * i1
            self.part[u(4 * h, 4)] = (
                self.own[u(mine, 4)].astype(F32)
                + self.near[u(8 * h, 4)].astype(F32)
                + self.near[u(8 * h + 4, 4)].astype(F32)
            ).astype(self.wide)
            for d in range(1, 4):
                self.go(
                    3, 2, self.part.at[u(4 * h + rem(i2 + d, 4), 1)], self.cross.at[u(3 * h + d - 1, 1)], peer2(d)
                )

    def s4(self):
        u = self.units
        self.got(2, self.cross, 6)
        for h, i1, peer1, i2, peer2 in self.halves():
            total = self.part[u(4 * h + i2, 1)].astype(F32)
            for d in range(1, 4):
                total = total + self.cross[u(3 * h + d - 1, 1)].astype(F32)
            self.pair[u(h, 1)] = total.astype(BF16)
            self.go(4, 3, self.pair.at[u(h, 1)], self.other.at[u(h, 1)], self.pair_id)

    def s5(self):
        u = self.units
        self.got(3, self.other, 2)
        for h, i1, peer1, i2, peer2 in self.halves():
            mine = u(16 * h + 4 * i1 + i2, 1)
            self.full[mine] = (self.pair[u(h, 1)].astype(F32) + self.other[u(h, 1)].astype(F32)).astype(BF16)
            for d in range(1, 4):
                self.go(5, 4, self.full.at[mine], self.full.at[mine], peer2(d))

    def sides(self):
        for h, i1, peer1, i2, peer2 in self.halves():
            low, high = (self.full.at[self.units(16 * h + 4 * i1 + at, 2)] for at in (0, 2))
            yield low, high, peer1

    def s6(self):
        self.got(4, self.full, 6)
        for low, high, peer1 in self.sides():
            self.go(6, 5, low, low, peer1(1))
            self.go(6, 5, high, high, peer1(3))

    def s6b(self):
        for low, high, peer1 in self.sides():
            self.go(7, 6, high, high, peer1(1))
            self.go(7, 6, low, low, peer1(3))

    def s7(self):
        u = self.units
        self.got(5, self.full, 8)
        for h, i1, peer1, i2, peer2 in self.halves():
            low = self.full.at[u(16 * h + 4 * rem(i1 + 3, 4), 2)]
            high = self.full.at[u(16 * h + 4 * rem(i1 + 1, 4) + 2, 2)]
            self.go(8, 6, low, low, peer1(1))
            self.go(8, 6, high, high, peer1(3))

    def s8(self):
        self.got(6, self.full, 16)


def pack(source, narrow, store, groups, ends):
    def body(q, carry):
        rows = pl.ds(pl.multiple_of(q * SUB, SUB), SUB)
        for g in groups:
            store(q, g, source[rows, LANES * g : LANES * (g + 1)].astype(BF16))
        return carry

    lax.fori_loop(0, 5, body, 0)
    narrow[:, :TAIL] = source[:, LAST]
    lane = lax.broadcasted_iota(jnp.int32, (TAILROWS, LANES), 1)
    packed = jnp.where(lane < TAIL, narrow[:TAILROWS, :], pltpu.roll(narrow[TAILROWS:, :], TAIL, 1))
    blank = jnp.zeros((4 * SUB - TAILROWS, LANES), F32)
    blocks = [packed[:SUB], packed[SUB : 2 * SUB], jnp.concatenate([packed[2 * SUB :], blank[:SUB // 2]], axis=0), blank[SUB // 2 :]]
    for g in ends:
        store(5, g, blocks[g].astype(BF16))


def tail(read):
    return jnp.concatenate([read(60), read(61), read(62)[: TAILROWS - 2 * SUB]], axis=0)


def kernel(
    w_hbm, m_hbm, tok_hbm, tgt_hbm, bw_ref, avg_hbm, bl_hbm, bw_hbm, sum_hbm,
    tok, tgt, w, m, g, half, narrow, avg, bl, bw, tsend, trecv, lsem, osem, *sum_refs,
):
    rep, shard = lax.axis_index("rep"), lax.axis_index("shard")
    x, zl, y = rep // 8, rem(rep // 4, 2), rem(rep, 4)
    zh, core = shard // 2, rem(shard, 2)
    right = (rep, 2 * rem(zh + 1, 4) + core)
    left = (rep, 2 * rem(zh + 3, 4) + core)
    partner = (rep, 2 * zh + 1 - core)
    pair_id = (8 * x + 4 * (1 - zl) + y, shard)

    def along_x(d):
        return (8 * rem(x + d, 4) + 4 * zl + y, shard)

    def along_y(d):
        return (8 * x + 4 * zl + rem(y + d, 4), shard)

    place = (((x, along_x), (y, along_y)), pair_id)
    per = len(Sum.sizes) + 2
    first = Sum(sum_refs[:per], place, 2, F32)
    second = Sum(sum_refs[per : 2 * per], place, 2, BF16)
    even = Sum(sum_refs[2 * per : 3 * per], place, 1, BF16)
    odd = Sum(sum_refs[3 * per :], place, 1, BF16)

    def into(total):
        def store(q, g, block):
            total.own[GROUPS * q + g] = block

        return store

    def into_half(total):
        def store(q, g, block):
            total.own[GROUPS // 2 * q + g // 2] = block

        return store


    loads = [
        pltpu.make_async_copy(tok_hbm.at[0], tok.at[0, 0, core], lsem.at[0]),
        pltpu.make_async_copy(w_hbm, w, lsem.at[1]),
        pltpu.make_async_copy(m_hbm, m, lsem.at[2]),
        pltpu.make_async_copy(tgt_hbm, tgt, lsem.at[3]),
        pltpu.make_async_copy(tok_hbm.at[1], tok.at[1, 0, core], lsem.at[4]),
    ]
    for load in loads:
        load.start()

    peers = [right, left, partner, pair_id] + [f(d) for f in (along_x, along_y) for d in (1, 2, 3)]
    barrier = pltpu.get_barrier_semaphore()
    for peer in peers:
        pl.semaphore_signal(barrier, inc=1, device_id=peer, device_id_type=MESH)
    pl.semaphore_wait(barrier, len(peers))

    def move(step, relay, src, dst, recv, device):
        pltpu.make_async_remote_copy(
            src_ref=src,
            dst_ref=dst,
            send_sem=tsend.at[step, relay],
            recv_sem=recv,
            device_id=device,
            device_id_type=MESH,
        ).start()

    def drain(step, relay):
        everything = tok.at[step, 0, 0] if relay else tok.at[step, pl.ds(0, 3)]
        pltpu.make_async_remote_copy(
            src_ref=everything,
            dst_ref=everything,
            send_sem=tsend.at[step, relay],
            recv_sem=trecv.at[step, 0, 0, 0],
            device_id=partner,
            device_id_type=MESH,
        ).wait_send()

    def came(recv, dst):
        pltpu.make_async_remote_copy(
            src_ref=dst,
            dst_ref=dst,
            send_sem=tsend.at[0, 0],
            recv_sem=recv,
            device_id=partner,
            device_id_type=MESH,
        ).wait_recv()

    def send_own(step):
        lower, upper = tok.at[step, 0, core, 0], tok.at[step, 0, core, 1]
        for src, chip, part, device in (
            (lower, 1, 0, right), (upper, 2, 1, left), (upper, 1, 1, right), (lower, 2, 0, left),
        ):
            move(step, 0, src, tok.at[step, chip, core, part], trecv.at[step, chip, core, part], device)
        both = tok.at[step, 0, core]
        move(step, 0, both, both, trecv.at[step, 0, core, 0], partner)

    waves = {1: ((1, 0), (2, 1)), 2: ((1, 1), (2, 0)), 3: ((3, 0), (3, 1))}

    def receive(step, wave):
        for k, (chip, part) in enumerate(waves[wave]):
            here, recv = tok.at[step, chip, core, part], trecv.at[step, chip, core, part]
            came(recv, here)
            if wave == 1:
                move(step, 1, here, tok.at[step, 3, core, part], trecv.at[step, 3, core, part], (right, left)[k])
            move(step, 0, here, here, recv, partner)

    def receive_partner(step, wave):
        if wave == 0:
            came(trecv.at[step, 0, 1 - core, 0], tok.at[step, 0, 1 - core])
            return
        for chip, part in waves[wave]:
            came(trecv.at[step, chip, 1 - core, part], tok.at[step, chip, 1 - core, part])

    scaling = 1.0 / math.sqrt(D)
    root = math.sqrt(2.0 / math.pi)

    def compute(step, chip):
        block = jnp.concatenate([tok[step, chip, c].reshape(D, TOKS) for c in range(2)], axis=1)
        value = jnp.dot(half[...], block, preferred_element_type=F32) * scaling
        start = rem(zh + (0, 3, 1, 2)[chip], 4) * (2 * TOKS)
        wanted = tgt[step, :, pl.ds(pl.multiple_of(start, 2 * TOKS), 2 * TOKS)].astype(F32)
        square = value * value
        curve = jnp.tanh(root * value * (1.0 + 0.044715 * square))
        gate = 0.5 * (1.0 + curve)
        slope = gate + 0.5 * value * (1.0 - curve * curve) * (root * (1.0 + 3 * 0.044715 * square))
        grad = ((value * gate - wanted) * slope * scaling).astype(BF16)
        part = lax.dot_general(grad, block, (((1,), (1,)), ((), ())), preferred_element_type=F32)
        if chip == 0:
            g[...] = part
        else:
            g[...] += part

    share = 1.0 / REPS
    every, ends = range(GROUPS), range(4)
    loads[0].wait()
    send_own(0)
    loads[1].wait()
    half[...] = w[...].astype(BF16)
    pack(w, narrow, into(first), every, ends)
    first.s1()
    loads[2].wait()
    loads[3].wait()
    loads[4].wait()

    receive_partner(0, 0)
    compute(0, 0)
    first.s1b()
    first.s2()
    first.s3()
    first.s4()

    receive(0, 1)
    receive(0, 2)
    receive_partner(0, 1)
    receive_partner(0, 2)
    compute(0, 1)
    compute(0, 2)
    first.s5()
    drain(0, 1)
    send_own(1)

    receive(0, 3)
    first.s6()
    receive_partner(0, 3)
    compute(0, 3)
    first.s6b()
    m[...] = momentum_decay * m[...] + g[...]
    half[...] = (w[...] - learn_rate * m[...]).astype(BF16)
    pack(m, narrow, into(second), every, ends)
    second.s1()
    first.s7()

    receive_partner(1, 0)
    compute(1, 0)
    second.s1b()
    second.s2()
    second.s3()
    second.s4()

    receive(1, 1)
    receive(1, 2)
    receive_partner(1, 1)
    receive_partner(1, 2)
    compute(1, 1)
    first.s8()
    second.s5()
    compute(1, 2)
    second.s6()
    second.s6b()

    receive(1, 3)
    receive_partner(1, 3)
    compute(1, 3)
    pack(g, narrow, into_half(even), every[::2], ends[::2])
    even.s1()
    pack(g, narrow, into_half(odd), every[1::2], ends[1::2])
    even.flush()
    odd.s1()
    second.s7()
    odd.flush()
    even.s1b()
    odd.s1b()
    m[...] = momentum_decay * m[...] + g[...]
    even.s2()
    even.flush()
    odd.s2()
    second.s8()

    same = lax.broadcasted_iota(jnp.int32, (COLS, COLS), 0) == lax.broadcasted_iota(jnp.int32, (COLS, COLS), 1)
    column = jnp.sum(jnp.where(same, bw_ref[...], 0.0), axis=1, keepdims=True)
    bw[...] = jnp.broadcast_to(column, (COLS, LANES))

    def sums(block):
        w0 = first.full[block].astype(F32)
        m1 = second.full[block].astype(F32)
        average = w0 - (learn_rate * (1.0 + momentum_decay)) * m1
        return average * share, m1 * (momentum_decay * share)

    def base(q, carry):
        rows = pl.ds(pl.multiple_of(q * SUB, SUB), SUB)
        part = bw[rows, :]
        for k in range(GROUPS):
            columns = slice(LANES * k, LANES * (k + 1))
            average, mean = sums(GROUPS * q + k)
            avg[rows, columns] = average
            bl[rows, columns] = part * mean + (1.0 - part) * m[rows, columns]
        return carry

    lax.fori_loop(0, 5, base, 0)
    for b in range(2):
        rows = slice(TAILROWS * b, TAILROWS * (b + 1))
        average, mean = (tail(lambda block: sums(block)[k]) for k in range(2))
        if b:
            average, mean = pltpu.roll(average, TAIL, 1), pltpu.roll(mean, TAIL, 1)
        part = bw[rows, :TAIL]
        avg[rows, LAST] = average[:, :TAIL]
        bl[rows, LAST] = part * mean[:, :TAIL] + (1.0 - part) * m[rows, LAST]
    outs = [
        pltpu.make_async_copy(avg, avg_hbm, lsem.at[0]),
        pltpu.make_async_copy(bl, bl_hbm, lsem.at[1]),
        pltpu.make_async_copy(bw, bw_hbm, lsem.at[2]),
    ]
    for out in outs:
        out.start()

    even.s3()
    even.flush()
    odd.s3()
    even.s4()
    even.flush()
    odd.s4()
    even.s5()
    even.flush()
    odd.s5()
    even.s6()
    even.flush()
    odd.s6()
    odd.flush()
    even.s6b()
    odd.s6b()
    even.s7()
    odd.s7()
    even.s8()

    def store(k, total):
        for part in range(4):
            here = pl.ds(8 * part, 8)
            outs.append(pltpu.make_async_copy(total.full.at[here], sum_hbm.at[k, here], osem.at[k, part]))
            outs[-1].start()

    store(0, even)
    odd.s8()
    store(1, odd)
    def end_sends():
        drain(0, 0)
        drain(1, 0)
        drain(1, 1)
        for total in (first, second, even, odd):
            total.flush()

    def end_outs():
        for out in outs:
            out.wait()

    end_sends()
    end_outs()


def finish(avg_hbm, bl_hbm, bw_hbm, sum_hbm, avg_out, bl_out, avg, bl, bw, total, sem):
    rows = [pl.ds(SUB * q, SUB) for q in range(5)]
    small = [
        pltpu.make_async_copy(sum_hbm.at[:, pl.ds(30, 2)], total.at[:, pl.ds(30, 2)], sem.at[0]),
        pltpu.make_async_copy(bw_hbm, bw, sem.at[1]),
    ]
    loads = [
        [
            pltpu.make_async_copy(sum_hbm.at[:, pl.ds(6 * q, 6)], total.at[:, pl.ds(6 * q, 6)], sem.at[2 + q]),
            pltpu.make_async_copy(avg_hbm.at[rows[q]], avg.at[rows[q]], sem.at[7 + q]),
            pltpu.make_async_copy(bl_hbm.at[rows[q]], bl.at[rows[q]], sem.at[12 + q]),
        ]
        for q in range(5)
    ]
    for copy in small + sum(loads, []):
        copy.start()
    share = 1.0 / REPS
    for copy in small:
        copy.wait()
    ends = [tail(lambda block: total[block % 2, block // 2].astype(F32)) * share]
    ends.append(pltpu.roll(ends[0], TAIL, 1))
    outs = []
    for q in range(5):
        for copy in loads[q]:
            copy.wait()
        part = bw[rows[q], :] * share
        for k in range(GROUPS):
            columns = slice(LANES * k, LANES * (k + 1))
            value = total[k % 2, 6 * q + k // 2].astype(F32)
            avg[rows[q], columns] = avg[rows[q], columns] - (learn_rate * share) * value
            bl[rows[q], columns] = bl[rows[q], columns] + part * value
        for b in range(2):
            start, stop = max(SUB * q, TAILROWS * b), min(SUB * (q + 1), TAILROWS * (b + 1))
            if start < stop:
                here = slice(start, stop)
                value = ends[b][start - TAILROWS * b : stop - TAILROWS * b, :TAIL]
                avg[here, LAST] = avg[here, LAST] - learn_rate * value
                bl[here, LAST] = bl[here, LAST] + bw[here, :TAIL] * value
        for source, out, slot in ((avg, avg_out, 17 + q), (bl, bl_out, 22 + q)):
            outs.append(pltpu.make_async_copy(source.at[rows[q]], out.at[rows[q]], sem.at[slot]))
            outs[-1].start()
    for out in outs:
        out.wait()


def local(params, momentum, tokens, targets, blend_weight):
    anywhere = pl.BlockSpec(memory_space=pl.ANY)
    whole = jax.ShapeDtypeStruct((COLS, D), F32)
    parts = pl.pallas_call(
        kernel,
        out_shape=[
            whole,
            whole,
            jax.ShapeDtypeStruct((COLS, LANES), F32),
            jax.ShapeDtypeStruct((2, 32, SUB, LANES), BF16),
        ],
        in_specs=[anywhere] * 4 + [pl.BlockSpec(memory_space=pltpu.VMEM)],
        out_specs=[anywhere] * 4,
        scratch_shapes=[
            pltpu.VMEM((2, 4, 2, 2, D // 2, TOKS), BF16),
            pltpu.VMEM((2, COLS, 1024), BF16),
            pltpu.VMEM((COLS, D), F32),
            pltpu.VMEM((COLS, D), F32),
            pltpu.VMEM((COLS, D), F32),
            pltpu.VMEM((COLS, D), BF16),
            pltpu.VMEM((COLS, LANES), F32),
            pltpu.VMEM((COLS, D), F32),
            pltpu.VMEM((COLS, D), F32),
            pltpu.VMEM((COLS, LANES), F32),
            pltpu.SemaphoreType.DMA((2, 2)),
            pltpu.SemaphoreType.DMA((2, 4, 2, 2)),
            pltpu.SemaphoreType.DMA((5,)),
            pltpu.SemaphoreType.DMA((2, 4)),
            *Sum.scratch(2, F32),
            *Sum.scratch(2, BF16),
            *Sum.scratch(1, BF16),
            *Sum.scratch(1, BF16),
        ],
        compiler_params=pltpu.CompilerParams(
            collective_id=0, has_side_effects=True, vmem_limit_bytes=67043328
        ),
        name="window",
    )(
        params[0].T,
        momentum[0].T,
        tokens[0].transpose(0, 2, 1).reshape(2, 2, D // 2, TOKS),
        targets[0].transpose(0, 2, 1),
        blend_weight.reshape(1, COLS),
    )
    averaged, blended = pl.pallas_call(
        finish,
        out_shape=[whole, whole],
        in_specs=[anywhere] * 4,
        out_specs=[anywhere] * 2,
        scratch_shapes=[
            pltpu.VMEM((COLS, D), F32),
            pltpu.VMEM((COLS, D), F32),
            pltpu.VMEM((COLS, LANES), F32),
            pltpu.VMEM((2, 32, SUB, LANES), BF16),
            pltpu.SemaphoreType.DMA((27,)),
        ],
        name="finish",
    )(*parts)
    return averaged.T, blended.T[None]


def solution(mesh):
    return jax.shard_map(
        local,
        mesh=mesh,
        in_specs=(
            P("rep", None, "shard"),
            P("rep", None, "shard"),
            P("rep", None, "shard", None),
            P("rep", None, None, "shard"),
            P("shard"),
        ),
        out_specs=(P(None, "shard"), P("rep", None, "shard")),
        check_vma=False,
    )
```

time: 499 us -> 113 us (0.23)
  waiting for transfers between devices: 415 us -> 0 us
  Pallas kernels: 0 us -> 111 us
  local copies, waits for them, and re-layouts: 35.1 us -> 0 us
  matrix products: 22.2 us -> 0 us
  between operations: 13.8 us -> 0.8 us
  other arithmetic: 11.9 us -> 0 us
    all_gather x2 -> x0, waiting for transfers between devices: 246 us -> none  [the longest x1 165 us: in_one_piece(): lax.all_gather(both, axis, axis=dim, tiled=True)]
    reduce_scatter x1 -> x0, waiting for transfers between devices: 169 us -> none  [sum_together(): lax.psum_scatter(lines, axis, tiled=True).reshape(-1)]
    pallas_call x0 -> x2, Pallas kernels: none -> 111 us  [the longest x1 106 us: local(): pl.pallas_call(kernel, out_shape=[whole, whole, jax.ShapeDtypeStruct((COL...]
    dot_general x2 -> x0, matrix products: 22.2 us -> none  [local(): lax.dot_general(inputs[local_step], hidden_grad, (((0,), (0,)), ((), ()))...]
    unnamed x7 -> x0, local copies, waits for them, and re-layouts: 13 us -> none
    concatenate x1 -> x0, other arithmetic: 5.67 us -> none  [sum_together(): lines = jnp.concatenate([b.reshape(count, -1) for b in parts], axis=1)]
    split x1 -> x0, local copies, waits for them, and re-layouts: 5.62 us -> none  [in_one_piece(): jnp.split(lax.all_gather(both, axis, axis=dim, tiled=True), ends, axis=al...]
    reshape x1 -> x0, local copies, waits for them, and re-layouts: 5.53 us -> none  [sum_together(): jnp.pad(lines, ((0, 0), (0, rows * 128 - lines.shape[1]))).reshape(-1, 128)]
  transfers between devices with their start and end apart: 3 -> 0, of which waited for: 3 -> 0; matrix products, arithmetic and copies ran while one was open for 0% -> 0% of each run, Pallas kernels for 0% -> 0%
where the time goes in v2:
time: 113 us; the launch traced here: 112 us
  Pallas kernels  111 us (98%)
    pallas_call x1, Pallas kernels, local(): pl.pallas_call(kernel, out_shape=[whole, whole, jax.ShapeDtypeStruct((COL...  106 us
    pallas_call x1, Pallas kernels, local(): pl.pallas_call(finish, out_shape=[whole, whole], in_specs=[anywhere] * 4,...  5.56 us

profile of v2, /device:TPU:8, one launch (start us, length us, event | category | flops | bytes accessed | tf_op | source)
XLA Modules:
  0.0 111.9 jit_solution(456569060808601528)
XLA Ops:
  0.6 105.5 %window.1 = (f32[400,1600]{1,0:T(8,128)}, f32[400,1600]{1,0:T(8,128)}, f32[400,128]{1,0:T(8,128)}, bf16[2,32,80,128]{3,2,1,0:T(8,128)(2,1)}) custom-call(f32[400,1600]{1,0:T(8,128)} %bitcast.19, f32[400,1600]{1,0:T(8,128)} %bitcast.20, bf16[2,2,800,128]{3,2,1,0:T(8,128)(2,1)} %bitcast.22, bf16[2,400,1024]{2,1,0:T(8,128)(2,1)} %bitcast.21, f32[1,400]{1,0:T(1,128)} %bitcast.23), custom_call_target="tpu_custom_call" | custom-call | tf_op jit(solution)/shard_map/window/pallas_call | solution.py:532
  106.1 5.6 %finish.1 = (f32[400,1600]{1,0:T(8,128)}, f32[400,1600]{1,0:T(8,128)}) custom-call(f32[400,1600]{1,0:T(8,128)} %get-tuple-element.8.avg_hbm, f32[400,1600]{1,0:T(8,128)} %get-tuple-element.9.bl_hbm, f32[400,128]{1,0:T(8,128)} %get-tuple-element.10.bw_hbm, bf16[2,32,80,128]{3,2,1,0:T(8,128)(2,1)} %get-tuple-element.11.sum_hbm), custom_call_target="tpu_custom_call" | custom-call | tf_op jit(solution)/shard_map/finish/pallas_call | solution.py:573

commit v3 on v2

--- a/solution.py
+++ b/solution.py
@@ -280,14 +280,14 @@
             device_id_type=MESH,
         ).wait_recv()
 
-    def send_own(step):
+    def send_own(step, turn):
         lower, upper = tok.at[step, 0, core, 0], tok.at[step, 0, core, 1]
-        for src, chip, part, device in (
-            (lower, 1, 0, right), (upper, 2, 1, left), (upper, 1, 1, right), (lower, 2, 0, left),
-        ):
+        turns = (((lower, 1, 0, right), (upper, 2, 1, left)), ((upper, 1, 1, right), (lower, 2, 0, left)))
+        for src, chip, part, device in turns[turn]:
             move(step, 0, src, tok.at[step, chip, core, part], trecv.at[step, chip, core, part], device)
-        both = tok.at[step, 0, core]
-        move(step, 0, both, both, trecv.at[step, 0, core, 0], partner)
+        if turn == 0:
+            both = tok.at[step, 0, core]
+            move(step, 0, both, both, trecv.at[step, 0, core, 0], partner)
 
     waves = {1: ((1, 0), (2, 1)), 2: ((1, 1), (2, 0)), 3: ((3, 0), (3, 1))}
 
@@ -328,7 +328,7 @@
     share = 1.0 / REPS
     every, ends = range(GROUPS), range(4)
     loads[0].wait()
-    send_own(0)
+    send_own(0, 0)
     loads[1].wait()
     half[...] = w[...].astype(BF16)
     pack(w, narrow, into(first), every, ends)
@@ -338,52 +338,51 @@
     loads[4].wait()
 
     receive_partner(0, 0)
+    send_own(0, 1)
+    first.s1b()
     compute(0, 0)
-    first.s1b()
     first.s2()
     first.s3()
+
+    receive(0, 1)
     first.s4()
-
-    receive(0, 1)
     receive(0, 2)
     receive_partner(0, 1)
     receive_partner(0, 2)
     compute(0, 1)
     compute(0, 2)
+    drain(0, 1)
+    send_own(1, 0)
     first.s5()
-    drain(0, 1)
-    send_own(1)
 
     receive(0, 3)
-    first.s6()
     receive_partner(0, 3)
     compute(0, 3)
-    first.s6b()
+    send_own(1, 1)
     m[...] = momentum_decay * m[...] + g[...]
     half[...] = (w[...] - learn_rate * m[...]).astype(BF16)
     pack(m, narrow, into(second), every, ends)
     second.s1()
-    first.s7()
 
     receive_partner(1, 0)
     compute(1, 0)
     second.s1b()
     second.s2()
     second.s3()
+
+    receive(1, 1)
+    first.s6()
+    first.s6b()
     second.s4()
-
-    receive(1, 1)
     receive(1, 2)
+    first.s7()
     receive_partner(1, 1)
     receive_partner(1, 2)
     compute(1, 1)
-    first.s8()
+    compute(1, 2)
+
+    receive(1, 3)
     second.s5()
-    compute(1, 2)
-    second.s6()
-    second.s6b()
-
-    receive(1, 3)
     receive_partner(1, 3)
     compute(1, 3)
     pack(g, narrow, into_half(even), every[::2], ends[::2])
@@ -391,7 +390,6 @@
     pack(g, narrow, into_half(odd), every[1::2], ends[1::2])
     even.flush()
     odd.s1()
-    second.s7()
     odd.flush()
     even.s1b()
     odd.s1b()
@@ -399,6 +397,22 @@
     even.s2()
     even.flush()
     odd.s2()
+    even.s3()
+    odd.s3()
+    second.s6()
+    second.s6b()
+    even.s4()
+    odd.s4()
+    even.s5()
+    odd.s5()
+    second.s7()
+    even.s6()
+    even.flush()
+    odd.s6()
+    odd.flush()
+    even.s6b()
+    odd.s6b()
+    first.s8()
     second.s8()
 
     same = lax.broadcasted_iota(jnp.int32, (COLS, COLS), 0) == lax.broadcasted_iota(jnp.int32, (COLS, COLS), 1)
@@ -438,21 +452,6 @@
     for out in outs:
         out.start()
 
-    even.s3()
-    even.flush()
-    odd.s3()
-    even.s4()
-    even.flush()
-    odd.s4()
-    even.s5()
-    even.flush()
-    odd.s5()
-    even.s6()
-    even.flush()
-    odd.s6()
-    odd.flush()
-    even.s6b()
-    odd.s6b()
     even.s7()
     odd.s7()
     even.s8()

time: 113 us -> 107 us (0.947)
  Pallas kernels: 111 us -> 106 us
    pallas_call x1, Pallas kernels: 106 us -> 100 us  [local(): pl.pallas_call(kernel, out_shape=[whole, whole, jax.ShapeDtypeStruct((COL...]
where the time goes in v3:
time: 107 us
  Pallas kernels  106 us (99%)
    pallas_call x1, Pallas kernels, local(): pl.pallas_call(kernel, out_shape=[whole, whole, jax.ShapeDtypeStruct((COL...  100 us
    pallas_call x1, Pallas kernels, local(): pl.pallas_call(finish, out_shape=[whole, whole], in_specs=[anywhere] * 4,...  5.56 us

profile of v3, /device:TPU:8, one launch (start us, length us, event | category | flops | bytes accessed | tf_op | source)
XLA Modules:
  0.0 106.6 jit_solution(12838431569325586989)
XLA Ops:
  0.6 100.2 %window.1 = (f32[400,1600]{1,0:T(8,128)}, f32[400,1600]{1,0:T(8,128)}, f32[400,128]{1,0:T(8,128)}, bf16[2,32,80,128]{3,2,1,0:T(8,128)(2,1)}) custom-call(f32[400,1600]{1,0:T(8,128)} %bitcast.19, f32[400,1600]{1,0:T(8,128)} %bitcast.20, bf16[2,2,800,128]{3,2,1,0:T(8,128)(2,1)} %bitcast.22, bf16[2,400,1024]{2,1,0:T(8,128)(2,1)} %bitcast.21, f32[1,400]{1,0:T(1,128)} %bitcast.23), custom_call_target="tpu_custom_call" | custom-call | tf_op jit(solution)/shard_map/window/pallas_call | solution.py:531
  100.9 5.6 %finish.1 = (f32[400,1600]{1,0:T(8,128)}, f32[400,1600]{1,0:T(8,128)}) custom-call(f32[400,1600]{1,0:T(8,128)} %get-tuple-element.8.avg_hbm, f32[400,1600]{1,0:T(8,128)} %get-tuple-element.9.bl_hbm, f32[400,128]{1,0:T(8,128)} %get-tuple-element.10.bw_hbm, bf16[2,32,80,128]{3,2,1,0:T(8,128)(2,1)} %get-tuple-element.11.sum_hbm), custom_call_target="tpu_custom_call" | custom-call | tf_op jit(solution)/shard_map/finish/pallas_call | solution.py:572

commit v4 on v3

--- a/solution.py
+++ b/solution.py
@@ -368,9 +368,9 @@
     compute(1, 0)
     second.s1b()
     second.s2()
+
+    receive(1, 1)
     second.s3()
-
-    receive(1, 1)
     first.s6()
     first.s6b()
     second.s4()
@@ -388,14 +388,13 @@
     pack(g, narrow, into_half(even), every[::2], ends[::2])
     even.s1()
     pack(g, narrow, into_half(odd), every[1::2], ends[1::2])
+    odd.s1()
+    m[...] = momentum_decay * m[...] + g[...]
     even.flush()
-    odd.s1()
     odd.flush()
     even.s1b()
     odd.s1b()
-    m[...] = momentum_decay * m[...] + g[...]
     even.s2()
-    even.flush()
     odd.s2()
     even.s3()
     odd.s3()
@@ -407,11 +406,7 @@
     odd.s5()
     second.s7()
     even.s6()
-    even.flush()
     odd.s6()
-    odd.flush()
-    even.s6b()
-    odd.s6b()
     first.s8()
     second.s8()
 
@@ -452,6 +447,8 @@
     for out in outs:
         out.start()
 
+    even.s6b()
+    odd.s6b()
     even.s7()
     odd.s7()
     even.s8()

time: 107 us -> 105 us (0.981)
  Pallas kernels: 106 us -> 104 us
    pallas_call x1, Pallas kernels: 100 us -> 98 us  [local(): pl.pallas_call(kernel, out_shape=[whole, whole, jax.ShapeDtypeStruct((COL...]
where the time goes in v4:
time: 105 us; the launch traced here: 104 us
  Pallas kernels  104 us (99%)
    pallas_call x1, Pallas kernels, local(): pl.pallas_call(kernel, out_shape=[whole, whole, jax.ShapeDtypeStruct((COL...  98 us
    pallas_call x1, Pallas kernels, local(): pl.pallas_call(finish, out_shape=[whole, whole], in_specs=[anywhere] * 4,...  5.56 us

profile of v4, /device:TPU:8, one launch (start us, length us, event | category | flops | bytes accessed | tf_op | source)
XLA Modules:
  0.0 104.3 jit_solution(5852012276406322586)
XLA Ops:
  0.6 98.0 %window.1 = (f32[400,1600]{1,0:T(8,128)}, f32[400,1600]{1,0:T(8,128)}, f32[400,128]{1,0:T(8,128)}, bf16[2,32,80,128]{3,2,1,0:T(8,128)(2,1)}) custom-call(f32[400,1600]{1,0:T(8,128)} %bitcast.19, f32[400,1600]{1,0:T(8,128)} %bitcast.20, bf16[2,2,800,128]{3,2,1,0:T(8,128)(2,1)} %bitcast.22, bf16[2,400,1024]{2,1,0:T(8,128)(2,1)} %bitcast.21, f32[1,400]{1,0:T(1,128)} %bitcast.23), custom_call_target="tpu_custom_call" | custom-call | tf_op jit(solution)/shard_map/window/pallas_call | solution.py:528
  98.6 5.6 %finish.1 = (f32[400,1600]{1,0:T(8,128)}, f32[400,1600]{1,0:T(8,128)}) custom-call(f32[400,1600]{1,0:T(8,128)} %get-tuple-element.8.avg_hbm, f32[400,1600]{1,0:T(8,128)} %get-tuple-element.9.bl_hbm, f32[400,128]{1,0:T(8,128)} %get-tuple-element.10.bw_hbm, bf16[2,32,80,128]{3,2,1,0:T(8,128)(2,1)} %get-tuple-element.11.sum_hbm), custom_call_target="tpu_custom_call" | custom-call | tf_op jit(solution)/shard_map/finish/pallas_call | solution.py:569
